TPU v7x, 32 devices: a whole 2x2x4 slice. The times are simulated.
32 devices in a mesh: row: 8 (over z, y), col: 4 (over x, core).
Axes of the slice: x: 2, y: 2, z: 4, core: 2. Of those that a mesh axis runs over, the one named last changes fastest.
Arguments:
- layer_input: bfloat16 [2048, 8192], P('row'), may hold values from -7 to 7
- gain: float32 [8192], replicated, may hold values from 0.5 to 6
- d_query: bfloat16 [2048, 4096], P('row', 'col'), may hold values from -6 to 6
- d_keyval: bfloat16 [2048, 2048], P('row', 'col'), may hold values from -6 to 6
- w_query: bfloat16 [8192, 4096], P('row', 'col'), may hold values from -0.0625 to 0.0625
- w_keyval: bfloat16 [8192, 2048], P('row', 'col'), may hold values from -1 to 1
- d_resid: bfloat16 [2048, 8192], P('row', 'col'), may hold values from -6 to 6
Outputs:
- d_input: bfloat16 [2048, 8192], P('row', 'col')
- grad_wq: bfloat16 [8192, 4096], P('row', 'col')
- grad_wkv: bfloat16 [8192, 2048], P('row', 'col')
- grad_gain: float32 [8192], P('col')
- grad_square_sum: float32 [], replicated
All inputs are finite; a program needn't handle non-finite values.
Results may differ from a plain program's by a relative error of at most 0.023.
Values may be sent and summed in bfloat16 or wider, within the bound.
A program may use at most 128 MiB of HBM per device.

v0:
```python
import math
import jax
import jax.numpy as jnp
from jax import lax
from jax.sharding import PartitionSpec as P

epsilon = 1e-05


def local(layer_input, gain, d_query, d_keyval, w_query, w_keyval, d_resid):
    inputs = layer_input.astype(jnp.float32)
    inv_rms = lax.rsqrt(jnp.mean(inputs * inputs, axis=1, keepdims=True) + epsilon)
    normed = (inputs * inv_rms * gain).astype(jnp.bfloat16)
    model_width = inputs.shape[1]
    local_tokens = inputs.shape[0]
    tokens_all = local_tokens * lax.axis_size("row")
    scaling = 1.0 / math.sqrt(tokens_all)
    weight_scale = 1.0 / math.sqrt(local_tokens)
    contract_cols = (((1,), (1,)), ((), ()))
    query_cols = d_query.shape[1]
    cotangent = jnp.concatenate([d_query, d_keyval], axis=1)
    all_cotangents = lax.all_gather(cotangent, "row", axis=0, tiled=True)
    weights = jnp.concatenate([w_query, w_keyval], axis=1)
    partial_value = lax.dot_general(
        all_cotangents, weights, contract_cols, preferred_element_type=jnp.float32
    )
    reduced = lax.psum_scatter(
        partial_value.astype(jnp.bfloat16), "col", scatter_dimension=0, tiled=True
    )
    n_row, n_col = (lax.axis_size("row"), lax.axis_size("col"))
    fold = n_row // n_col
    pieces = reduced.reshape(fold, local_tokens, reduced.shape[1])
    row, col = (lax.axis_index("row"), lax.axis_index("col"))
    arrived = []
    for shift in range(fold):
        pairs = [
            (r * n_col + c, (fold * c + (r + shift) % fold) * n_col + r // fold)
            for r in range(n_row)
            for c in range(n_col)
        ]
        piece = lax.dynamic_index_in_dim(pieces, (row + shift) % fold, 0, keepdims=False)
        arrived.append(lax.ppermute(piece, ("row", "col"), pairs))
    arrived = jnp.stack(arrived)
    feature_grad = jnp.concatenate(
        [
            lax.dynamic_index_in_dim(arrived, (row - j + fold) % fold, 0, keepdims=False)
            for j in range(fold)
        ],
        axis=1,
    ).astype(jnp.float32)
    slice_width = feature_grad.shape[1]
    col_start = lax.axis_index("col") * slice_width
    input_part = lax.dynamic_slice_in_dim(inputs, col_start, slice_width, 1)
    gain_part = lax.dynamic_slice_in_dim(gain, col_start, slice_width, 0)
    weighted = gain_part * feature_grad
    token_dot = lax.psum(jnp.sum(weighted * input_part, axis=1, keepdims=True), "col")
    d_input = (
        d_resid.astype(jnp.float32)
        + inv_rms * weighted
        - input_part * inv_rms**3 * token_dot / model_width
    ).astype(jnp.bfloat16)
    gain_partial = jnp.sum(feature_grad * input_part * inv_rms, axis=0) * scaling
    cotangent = jnp.concatenate([d_query, d_keyval], axis=1)
    columns = lax.all_to_all(normed, "row", split_axis=1, concat_axis=0, tiled=True)
    groups = lax.axis_size("row")
    column_blocks = columns.reshape(groups, local_tokens, columns.shape[1])
    grad_blocks = all_cotangents.reshape(groups, local_tokens, all_cotangents.shape[1])
    blocks = (
        lax.dot_general(
            column_blocks,
            grad_blocks,
            (((1,), (1,)), ((0,), (0,))),
            preferred_element_type=jnp.float32,
        )
        * weight_scale
    )
    summed = jnp.sum(blocks.astype(jnp.bfloat16).astype(jnp.float32), axis=0)
    grad_wq = summed[:, :query_cols].astype(jnp.bfloat16)
    grad_wkv = summed[:, query_cols:].astype(jnp.bfloat16)
    query_f = grad_wq.astype(jnp.float32)
    keyval_f = grad_wkv.astype(jnp.float32)
    tile_square = jnp.sum(query_f * query_f) + jnp.sum(keyval_f * keyval_f)
    grad_gain = lax.psum(gain_partial, "row")
    leading = jnp.where(
        lax.axis_index("row") == 0, jnp.sum(grad_gain * grad_gain), jnp.float32(0.0)
    )
    grand_total = lax.psum(tile_square + leading, ("row", "col"))
    grad_square_sum = grand_total / jnp.float32(model_width)
    return (d_input, grad_wq, grad_wkv, grad_gain, grad_square_sum)


def solution(mesh):
    placed = (
        P("row", None),
        P(),
        P("row", "col"),
        P("row", "col"),
        P("row", "col"),
        P("row", "col"),
        P("row", "col"),
    )
    return jax.shard_map(
        local,
        mesh=mesh,
        in_specs=placed,
        out_specs=(P("row", "col"), P("row", "col"), P("row", "col"), P("col"), P()),
        check_vma=False,
    )
```

profile of v0, /device:TPU:13, one launch (start us, length us, event | category | flops | bytes accessed | tf_op | source)
XLA Modules:
  0.0 376.0 jit_solution(1316032979656445743)
XLA Ops:
  7.2 2.1 pad_maximum_fusion.1
  9.3 3.3 multiply_reduce_fusion
  12.6 0.2 copy-done
  12.8 3.1 multiply_convert_fusion.1
  15.9 6.5 %copy.12 = bf16[256,8192]{0,1:T(8,128)(2,1)} copy(bf16[256,8192]{1,0:T(8,128)(2,1)} %multiply_convert_fusion.1) | data formatting | bytes 8388608 | tf_op jit(solution)/shard_map/convert_element_type | solution.py:13
  22.3 5.8 %all-to-all-start = ((bf16[256,8,1024]{0,2,1:T(8,128)(2,1)}), bf16[256,8,1024]{0,2,1:T(8,128)(2,1)}, u32[]{:S(2)}, u32[]{:S(2)}) async-start(bf16[256,8,1024]{0,2,1:T(8,128)(2,1)} %bitcast.18), calls=%async_computation.1 | async-start | bytes 8388608 | tf_op jit(solution)/shard_map/all_to_all | solution.py:64
  28.1 150.8 %all-gather.2.cloned.1.call-done = bf16[2048,1536]{1,0:T(8,128)(2,1)} async-done(((bf16[256,1536]{1,0:T(8,128)(2,1)}), bf16[2048,1536]{1,0:T(8,128)(2,1)}) %all-gather.2.cloned.1.call-update) | async-done | bytes 6291472 | tf_op jit(solution)/shard_map/all_gather | solution.py:22
  179.0 10.4 %convolution_convert_fusion = bf16[2048,1024]{1,0:T(8,128)(2,1)} fusion(bf16[2048,1536]{1,0:T(8,128)(2,1)} %all-gather.2.cloned.1.call-done, bf16[1024,512]{1,0:T(8,128)(2,1)} %param.12, bf16[1024,1024]{1,0:T(8,128)(2,1)S(1)} %copy-done.4), kind=kOutput, calls=%fused_computation.6 | convolution fusion | flops 6450839552 | bytes 13631488 | tf_op jit(solution)/shard_map/dot_general | solution.py:24
  189.5 6.4 %convert_element_type.33 = f32[256,8192]{1,0:T(8,128)} convert(bf16[256,8192]{1,0:T(8,128)(2,1)} %param.7) | non-fusion elementwise | flops 2097152 | bytes 12582912 | tf_op jit(solution)/shard_map/convert_element_type | solution.py:11
  195.9 10.9 %fusion = bf16[1024,1536]{1,0:T(8,128)(2,1)S(1)} fusion(bf16[8,256,1536]{2,1,0:T(8,128)(2,1)} %bitcast.20, bf16[256,8,1024]{0,2,1:T(8,128)(2,1)} %all-to-all-done), kind=kOutput, calls=%fused_computation.3 | convolution fusion | flops 6478626816 | bytes 13631488 | tf_op jit(solution)/shard_map/dot_general | solution.py:69
  206.8 36.0 %reduce-scatter.2.cloned.1.call-done = bf16[512,1024]{1,0:T(8,128)(2,1)} async-done(((bf16[2048,1024]{1,0:T(8,128)(2,1)}), bf16[512,1024]{1,0:T(8,128)(2,1)}) %reduce-scatter.2.cloned.1.call-update) | async-done | bytes 1048592 | tf_op jit(solution)/shard_map/reduce_scatter | solution.py:27
  242.8 2.3 dynamic-slice_bitcast_fusion
  245.1 0.3 collective-permute-start.1
  245.3 5.3 %collective-permute-start = (bf16[256,1024]{1,0:T(8,128)(2,1)}, bf16[256,1024]{1,0:T(8,128)(2,1)}, u32[]{:S(2)}, u32[]{:S(2)}) collective-permute-start(bf16[256,1024]{1,0:T(8,128)(2,1)} %get-tuple-element.14), channel_id=1, source_target_pairs={{0,0},{1,8},{2,16},{3,24},{4,4},{5,12},{6,20},{7,28},{8,1},{9,9},{... | collective-permute-start | bytes 1572872 | tf_op jit(solution)/shard_map/ppermute | solution.py:42
  250.7 2.0 multiply_reduce_fusion.2
  252.7 2.9 multiply_reduce_fusion.1
  257.1 2.3 collective-permute-done.1
  259.3 1.6 fusion.16
  260.9 2.2 fusion.12
  263.2 47.4 %psum.22 = f32[2048]{0:T(1024)S(1)} all-reduce(f32[2048]{0:T(1024)S(1)} %broadcast_multiply_fusion), channel_id=1, replica_groups=mesh['row'=8,'col'=4] {'row'}, use_global_device_ids=true, to_apply=%region_6.7 | all-reduce | flops 2048 | bytes 16384 | tf_op jit(solution)/shard_map/psum | solution.py:83
  310.5 0.6 multiply_reduce_fusion.3
  311.8 45.0 %psum.23 = f32[]{:T(128)} all-reduce(f32[]{:T(128)S(6)} %add.80), channel_id=1, replica_groups=mesh['row'=8,'col'=4] {'row','col'}, use_global_device_ids=true, to_apply=%region_10.11 | all-reduce | flops 1 | bytes 8 | tf_op jit(solution)/shard_map/psum | solution.py:87
  356.8 7.3 %psum.21 = f32[256]{0:T(256)S(1)} all-reduce(f32[256]{0:T(256)S(1)} %get-tuple-element.6), channel_id=1, replica_groups=mesh['row'=8,'col'=4] {'col'}, use_global_device_ids=true, to_apply=%region_3.4 | all-reduce | flops 256 | bytes 2048 | tf_op jit(solution)/shard_map/psum | solution.py:56
  364.8 3.3 fusion.9
  (18 shorter events, 0.1 us)
Async XLA Ops:
  7.2 5.4 %copy-start.2 = (f32[8192]{0:T(1024)S(1)}, f32[8192]{0:T(1024)}, u32[]{:S(2)}) copy-start(f32[8192]{0:T(1024)} %param.8) | copy-start | bytes 98308
  7.2 171.8 %all-gather.2.cloned.1.call-start = ((), (), s32[]{:S(2)}) async-start(), calls=%async_computation.2 | async-start | bytes 7077888 | tf_op jit(solution)/shard_map/all_gather | solution.py:22
  9.3 3.5 copy-start
  22.3 156.6 %copy-start.4 = (bf16[1024,1024]{1,0:T(8,128)(2,1)S(1)}, bf16[1024,1024]{1,0:T(8,128)(2,1)}, u32[]{:S(2)}) copy-start(bf16[1024,1024]{1,0:T(8,128)(2,1)} %param.11) | copy-start | bytes 6291460
  22.3 173.5 %all-to-all-start = ((bf16[256,8,1024]{0,2,1:T(8,128)(2,1)}), bf16[256,8,1024]{0,2,1:T(8,128)(2,1)}, u32[]{:S(2)}, u32[]{:S(2)}) async-start(bf16[256,8,1024]{0,2,1:T(8,128)(2,1)} %bitcast.18), calls=%async_computation.1 | async-start | bytes 8388608 | tf_op jit(solution)/shard_map/all_to_all | solution.py:64
  28.1 214.7 %reduce-scatter.2.cloned.1.call-start = ((), (), s32[]{:S(2)}) async-start(), calls=%async_computation.3 | async-start | bytes 5242880 | tf_op jit(solution)/shard_map/reduce_scatter | solution.py:27
  245.1 14.3 %collective-permute-start.1 = (bf16[256,1024]{1,0:T(8,128)(2,1)}, bf16[256,1024]{1,0:T(8,128)(2,1)}, u32[]{:S(2)}, u32[]{:S(2)}) collective-permute-start(bf16[256,1024]{1,0:T(8,128)(2,1)} %get-tuple-element.13), channel_id=1, source_target_pairs={{0,4},{1,12},{2,20},{3,28},{4,0},{5,8},{6,16},{7,24},{8,5},{9,13},... | collective-permute-start | bytes 1572872 | tf_op jit(solution)/shard_map/ppermute | solution.py:42
  245.3 14.0 %collective-permute-start = (bf16[256,1024]{1,0:T(8,128)(2,1)}, bf16[256,1024]{1,0:T(8,128)(2,1)}, u32[]{:S(2)}, u32[]{:S(2)}) collective-permute-start(bf16[256,1024]{1,0:T(8,128)(2,1)} %get-tuple-element.14), channel_id=1, source_target_pairs={{0,0},{1,8},{2,16},{3,24},{4,4},{5,12},{6,20},{7,28},{8,1},{9,9},{... | collective-permute-start | bytes 1572872 | tf_op jit(solution)/shard_map/ppermute | solution.py:42
  255.7 109.1 %copy-start.1 = (bf16[256,2048]{1,0:T(8,128)(2,1)S(1)}, bf16[256,2048]{1,0:T(8,128)(2,1)}, u32[]{:S(2)}) copy-start(bf16[256,2048]{1,0:T(8,128)(2,1)} %param.13) | copy-start | bytes 3145732
  310.5 57.5 %copy-start.3 = (f32[2048]{0:T(1024)}, f32[2048]{0:T(1024)S(1)}, u32[]{:S(2)}) copy-start(f32[2048]{0:T(1024)S(1)} %psum.22) | copy-start | bytes 24580
Sparse Core Ops, SparseCore 0:
  10.7 168.1 all-gather.1
  189.5 53.2 reduce-scatter.1
where the time goes:
time: 377 us; the launch traced here: 376 us
  waiting for transfers between devices  189 us (50%)
  blocking collectives  99.7 us (26%)
  other arithmetic  27.5 us (7%)
  matrix products  21.3 us (6%)
  between operations  18 us (5%)
  starting transfers between devices  11.4 us (3%)
  local copies, waits for them, and re-layouts  8.96 us (2%)
    all_gather x1, waiting for transfers between devices, local(): all_cotangents = lax.all_gather(cotangent, 'row', axis=0, tiled=True)  151 us
    psum x1, blocking collectives, local(): grad_gain = lax.psum(gain_partial, 'row')  47.4 us
    psum x1, blocking collectives, local(): grand_total = lax.psum(tile_square + leading, ('row', 'col'))  45 us
    reduce_scatter x1, waiting for transfers between devices, local(): lax.psum_scatter(partial_value.astype(jnp.bfloat16), 'col', scatter_dimen...  36 us
    dot_general x1, matrix products, local(): lax.dot_general(column_blocks, grad_blocks, (((1,), (1,)), ((0,), (0,))),...  10.9 us
    dot_general x1, matrix products, local(): lax.dot_general(all_cotangents, weights, contract_cols, preferred_element...  10.4 us
  transfers between devices with their start and end apart: 5, of which 3 were waited for; matrix products, arithmetic and copies ran while one was open for 12% of the time, Pallas kernels for 0%

commit v1 on v0

--- a/solution.py
+++ b/solution.py
@@ -80,7 +80,7 @@
     query_f = grad_wq.astype(jnp.float32)
     keyval_f = grad_wkv.astype(jnp.float32)
     tile_square = jnp.sum(query_f * query_f) + jnp.sum(keyval_f * keyval_f)
-    grad_gain = lax.psum(gain_partial, "row")
+    grad_gain = jnp.sum(lax.all_gather(gain_partial, "row"), axis=0)
     leading = jnp.where(
         lax.axis_index("row") == 0, jnp.sum(grad_gain * grad_gain), jnp.float32(0.0)
     )

time: 377 us -> 389 us (1.032)
  blocking collectives: 99.7 us -> 111 us
    all_gather x0 -> x1, blocking collectives: none -> 56.9 us  [local(): grad_gain = jnp.sum(lax.all_gather(gain_partial, 'row'), axis=0)]
    psum x1 -> x0, blocking collectives: 47.4 us -> none  [local(): grad_gain = lax.psum(gain_partial, 'row')]
where the time goes in v1:
time: 389 us; the launch traced here: 387 us
  waiting for transfers between devices  189 us (49%)
  blocking collectives  111 us (29%)
  other arithmetic  27.5 us (7%)
  matrix products  21.3 us (5%)
  between operations  18 us (5%)
  starting transfers between devices  11.4 us (3%)
  local copies, waits for them, and re-layouts  8.98 us (2%)
    all_gather x1, waiting for transfers between devices, local(): all_cotangents = lax.all_gather(cotangent, 'row', axis=0, tiled=True)  151 us
    all_gather x1, blocking collectives, local(): grad_gain = jnp.sum(lax.all_gather(gain_partial, 'row'), axis=0)  56.9 us
    psum x1, blocking collectives, local(): grand_total = lax.psum(tile_square + leading, ('row', 'col'))  44.9 us
    reduce_scatter x1, waiting for transfers between devices, local(): lax.psum_scatter(partial_value.astype(jnp.bfloat16), 'col', scatter_dimen...  36 us
    dot_general x1, matrix products, local(): lax.dot_general(column_blocks, grad_blocks, (((1,), (1,)), ((0,), (0,))),...  10.9 us
    dot_general x1, matrix products, local(): lax.dot_general(all_cotangents, weights, contract_cols, preferred_element...  10.4 us
    psum x1, blocking collectives, local(): lax.psum(jnp.sum(weighted * input_part, axis=1, keepdims=True), 'col')  8.86 us
  transfers between devices with their start and end apart: 5, of which 3 were waited for; matrix products, arithmetic and copies ran while one was open for 12% of the time, Pallas kernels for 0%

profile of v1, /device:TPU:13, one launch (start us, length us, event | category | flops | bytes accessed | tf_op | source)
XLA Modules:
  0.0 387.1 jit_solution(4671930465909056214)
XLA Ops:
  7.2 2.1 pad_maximum_fusion.1
  9.3 3.3 multiply_reduce_fusion
  12.6 0.2 copy-done
  12.8 3.1 multiply_convert_fusion.1
  15.9 6.5 %copy.14 = bf16[256,8192]{0,1:T(8,128)(2,1)} copy(bf16[256,8192]{1,0:T(8,128)(2,1)} %multiply_convert_fusion.1) | data formatting | bytes 8388608 | tf_op jit(solution)/shard_map/convert_element_type | solution.py:13
  22.3 5.8 %all-to-all-start = ((bf16[256,8,1024]{0,2,1:T(8,128)(2,1)}), bf16[256,8,1024]{0,2,1:T(8,128)(2,1)}, u32[]{:S(2)}, u32[]{:S(2)}) async-start(bf16[256,8,1024]{0,2,1:T(8,128)(2,1)} %bitcast.18), calls=%async_computation.1 | async-start | bytes 8388608 | tf_op jit(solution)/shard_map/all_to_all | solution.py:64
  28.1 150.8 %all-gather.3.cloned.1.call-done = bf16[2048,1536]{1,0:T(8,128)(2,1)} async-done(((bf16[256,1536]{1,0:T(8,128)(2,1)}), bf16[2048,1536]{1,0:T(8,128)(2,1)}) %all-gather.3.cloned.1.call-update) | async-done | bytes 6291472 | tf_op jit(solution)/shard_map/all_gather | solution.py:22
  179.0 10.4 %convolution_convert_fusion = bf16[2048,1024]{1,0:T(8,128)(2,1)} fusion(bf16[2048,1536]{1,0:T(8,128)(2,1)} %all-gather.3.cloned.1.call-done, bf16[1024,512]{1,0:T(8,128)(2,1)} %param.12, bf16[1024,1024]{1,0:T(8,128)(2,1)S(1)} %copy-done.4), kind=kOutput, calls=%fused_computation.6 | convolution fusion | flops 6450839552 | bytes 13631488 | tf_op jit(solution)/shard_map/dot_general | solution.py:24
  189.5 6.4 %convert_element_type.33 = f32[256,8192]{1,0:T(8,128)} convert(bf16[256,8192]{1,0:T(8,128)(2,1)} %param.7) | non-fusion elementwise | flops 2097152 | bytes 12582912 | tf_op jit(solution)/shard_map/convert_element_type | solution.py:11
  195.9 10.9 %fusion = bf16[1024,1536]{1,0:T(8,128)(2,1)S(1)} fusion(bf16[8,256,1536]{2,1,0:T(8,128)(2,1)} %bitcast.20, bf16[256,8,1024]{0,2,1:T(8,128)(2,1)} %all-to-all-done), kind=kOutput, calls=%fused_computation.3 | convolution fusion | flops 6478626816 | bytes 13631488 | tf_op jit(solution)/shard_map/dot_general | solution.py:69
  206.8 36.0 %reduce-scatter.2.cloned.1.call-done = bf16[512,1024]{1,0:T(8,128)(2,1)} async-done(((bf16[2048,1024]{1,0:T(8,128)(2,1)}), bf16[512,1024]{1,0:T(8,128)(2,1)}) %reduce-scatter.2.cloned.1.call-update) | async-done | bytes 1048592 | tf_op jit(solution)/shard_map/reduce_scatter | solution.py:27
  242.8 2.3 dynamic-slice_bitcast_fusion
  245.1 0.3 collective-permute-start.1
  245.3 5.3 %collective-permute-start = (bf16[256,1024]{1,0:T(8,128)(2,1)}, bf16[256,1024]{1,0:T(8,128)(2,1)}, u32[]{:S(2)}, u32[]{:S(2)}) collective-permute-start(bf16[256,1024]{1,0:T(8,128)(2,1)} %get-tuple-element.14), channel_id=1, source_target_pairs={{0,0},{1,8},{2,16},{3,24},{4,4},{5,12},{6,20},{7,28},{8,1},{9,9},{... | collective-permute-start | bytes 1572872 | tf_op jit(solution)/shard_map/ppermute | solution.py:42
  250.7 2.0 multiply_reduce_fusion.2
  252.7 2.9 multiply_reduce_fusion.1
  257.1 2.3 collective-permute-done.1
  259.3 1.6 fusion.16
  260.9 2.2 fusion.12
  263.2 56.9 %all-gather = f32[16384]{0:T(1024)S(1)} all-gather(f32[2048]{0:T(1024)S(1)} %broadcast_multiply_fusion), channel_id=2, replica_groups=mesh['row'=8,'col'=4] {'row'}, dimensions={0}, use_global_device_ids=true | all-gather | bytes 73728 | tf_op jit(solution)/shard_map/all_gather | solution.py:83
  320.1 0.6 multiply_reduce_fusion.3
  321.4 8.9 %psum.14 = f32[256]{0:T(256)S(1)} all-reduce(f32[256]{0:T(256)S(1)} %get-tuple-element.6), channel_id=1, replica_groups=mesh['row'=8,'col'=4] {'col'}, use_global_device_ids=true, to_apply=%region_3.4 | all-reduce | flops 256 | bytes 2048 | tf_op jit(solution)/shard_map/psum | solution.py:56
  330.2 44.9 %psum.15 = f32[]{:T(128)} all-reduce(f32[]{:T(128)S(6)} %add.78), channel_id=1, replica_groups=mesh['row'=8,'col'=4] {'row','col'}, use_global_device_ids=true, to_apply=%region_10.11 | all-reduce | flops 1 | bytes 8 | tf_op jit(solution)/shard_map/psum | solution.py:87
  375.8 3.3 fusion.9
  (20 shorter events, 0.2 us)
Async XLA Ops:
  7.2 5.4 %copy-start.2 = (f32[8192]{0:T(1024)S(1)}, f32[8192]{0:T(1024)}, u32[]{:S(2)}) copy-start(f32[8192]{0:T(1024)} %param.8) | copy-start | bytes 98308
  7.2 171.8 %all-gather.3.cloned.1.call-start = ((), (), s32[]{:S(2)}) async-start(), calls=%async_computation.2 | async-start | bytes 7077888 | tf_op jit(solution)/shard_map/all_gather | solution.py:22
  9.3 3.5 copy-start
  22.3 156.6 %copy-start.4 = (bf16[1024,1024]{1,0:T(8,128)(2,1)S(1)}, bf16[1024,1024]{1,0:T(8,128)(2,1)}, u32[]{:S(2)}) copy-start(bf16[1024,1024]{1,0:T(8,128)(2,1)} %param.11) | copy-start | bytes 6291460
  22.3 173.5 %all-to-all-start = ((bf16[256,8,1024]{0,2,1:T(8,128)(2,1)}), bf16[256,8,1024]{0,2,1:T(8,128)(2,1)}, u32[]{:S(2)}, u32[]{:S(2)}) async-start(bf16[256,8,1024]{0,2,1:T(8,128)(2,1)} %bitcast.18), calls=%async_computation.1 | async-start | bytes 8388608 | tf_op jit(solution)/shard_map/all_to_all | solution.py:64
  28.1 214.7 %reduce-scatter.2.cloned.1.call-start = ((), (), s32[]{:S(2)}) async-start(), calls=%async_computation.3 | async-start | bytes 5242880 | tf_op jit(solution)/shard_map/reduce_scatter | solution.py:27
  245.1 14.3 %collective-permute-start.1 = (bf16[256,1024]{1,0:T(8,128)(2,1)}, bf16[256,1024]{1,0:T(8,128)(2,1)}, u32[]{:S(2)}, u32[]{:S(2)}) collective-permute-start(bf16[256,1024]{1,0:T(8,128)(2,1)} %get-tuple-element.13), channel_id=1, source_target_pairs={{0,4},{1,12},{2,20},{3,28},{4,0},{5,8},{6,16},{7,24},{8,5},{9,13},... | collective-permute-start | bytes 1572872 | tf_op jit(solution)/shard_map/ppermute | solution.py:42
  245.3 14.0 %collective-permute-start = (bf16[256,1024]{1,0:T(8,128)(2,1)}, bf16[256,1024]{1,0:T(8,128)(2,1)}, u32[]{:S(2)}, u32[]{:S(2)}) collective-permute-start(bf16[256,1024]{1,0:T(8,128)(2,1)} %get-tuple-element.14), channel_id=1, source_target_pairs={{0,0},{1,8},{2,16},{3,24},{4,4},{5,12},{6,20},{7,28},{8,1},{9,9},{... | collective-permute-start | bytes 1572872 | tf_op jit(solution)/shard_map/ppermute | solution.py:42
  255.7 120.1 %copy-start.1 = (bf16[256,2048]{1,0:T(8,128)(2,1)S(1)}, bf16[256,2048]{1,0:T(8,128)(2,1)}, u32[]{:S(2)}) copy-start(bf16[256,2048]{1,0:T(8,128)(2,1)} %param.13) | copy-start | bytes 3145732
  320.1 59.0 %copy-start.3 = (f32[2048]{0:T(1024)}, f32[2048]{0:T(1024)S(1)}, u32[]{:S(2)}) copy-start(f32[2048]{0:T(1024)S(1)} %reduce_sum.76) | copy-start | bytes 24580
Sparse Core Ops, SparseCore 0:
  10.7 168.1 all-gather.2
  189.5 53.2 reduce-scatter.1
